TPU v7x, 32 devices: a whole 2x2x4 slice. The times are simulated.
32 devices in a mesh: tm: 4 (over y, x), chan: 8 (over z, core).
Axes of the slice: x: 2, y: 2, z: 4, core: 2. Of those that a mesh axis runs over, the one named last changes fastest.
Arguments:
- samples: bfloat16 [1024, 131072], P('tm', 'chan'), may hold values from -6 to 6
- valid: int32 [1024, 16], P('tm', 'chan'), may hold values from 0 to 1, as said below
Outputs:
- average: float32 [1024, 4224], P(('tm', 'chan'))
Inputs may be any that keep to these rules, and one draw needn't show every extreme that they name: `valid`: split the channels into aligned groups of 256; in every segment each group has at most 192 entries equal to 1, and exactly 192 for some group and segment; at least one channel has no 1 in any segment.
All inputs are finite; a program needn't handle non-finite values.
Results may differ from a plain program's by a relative error of at most 0.0026.
Values may be sent and summed in bfloat16 or wider, within the bound.
No kernel may reach another device: no remote copies, remote signals or barrier semaphores. Data moves between devices by JAX's collectives and lax.ppermute only.
A program may use at most 128 MiB of HBM per device.

v0:
```python
import functools

import jax
import jax.numpy as jnp
import numpy as np
from jax import lax
from jax.experimental import pallas as pl
from jax.experimental.pallas import tpu as pltpu
from jax.sharding import PartitionSpec as P


RADIX = 128
KBANDS = 33
SUB = 8
HALF = RADIX // 2
STEP = HALF + 4
OUT = 72
ROWS = SUB * KBANDS + SUB
SEG = RADIX * RADIX
SLOTS = 6


def make_tables():
    counter = np.arange(RADIX)
    angle = 2 * np.pi * ((counter[:, None] * counter[None, :]) % RADIX) / RADIX
    cos, sin = np.cos(angle), np.sin(angle)
    first = np.block([[cos, -sin], [sin, cos]])
    mid = 2 * np.pi * (counter[:, None] * counter[None, :]) / SEG
    twiddle = np.stack([np.cos(mid), -np.sin(mid)])
    bands = np.concatenate([np.arange(KBANDS), RADIX - np.arange(KBANDS + 1)]) % RADIX
    second = np.zeros((2 * OUT, 2 * RADIX))
    size = len(bands)
    second[:size, :RADIX], second[:size, RADIX:] = cos[bands], sin[bands]
    second[OUT : OUT + size, :RADIX], second[OUT : OUT + size, RADIX:] = -sin[bands], cos[bands]
    window = (0.5 - 0.5 * np.cos(2 * np.pi * np.arange(SEG) / SEG)).astype(np.float32)
    mirror = np.zeros((RADIX, RADIX))
    mirror[(RADIX - counter) % RADIX, counter] = 1.0
    scale = np.full((KBANDS, RADIX), 2.0)
    scale[0, 0] = 1.0
    scale = 0.5 * scale / np.sum(window.astype(np.float64) ** 2)
    return (
        jnp.asarray(first, jnp.bfloat16),
        jnp.asarray(twiddle, jnp.float32),
        jnp.asarray(second, jnp.bfloat16),
        jnp.asarray(window.reshape(RADIX, RADIX)),
        jnp.asarray(mirror, jnp.bfloat16),
        jnp.asarray(scale, jnp.float32),
    )


def stage(dst, sums, source, half):
    total = [None] * 4
    for a in range(HALF):
        value = source[half * HALF + a].astype(jnp.float32)
        dst[pl.ds(a, SUB, stride=STEP), :] = value
        total[a % 4] = value if total[a % 4] is None else total[a % 4] + value
    total = (total[0] + total[1]) + (total[2] + total[3])
    sums[...] = jnp.broadcast_to(jnp.sum(total, axis=1, keepdims=True), (SUB, RADIX))


def shape(c, piece, window_ref):
    head, tail, head_sum, tail_sum, mask = piece
    rows = slice(c * STEP, c * STEP + HALF)
    value = jnp.concatenate([head[rows, :], tail[rows, :]], axis=0)
    mean = (head_sum[c : c + 1, :] + tail_sum[c : c + 1, :]) * (1.0 / SEG)
    shaped = ((value - mean) * window_ref[...]).astype(jnp.bfloat16)
    return (shaped * mask[c : c + 1, :].astype(jnp.bfloat16)).T


def pair_power(lhs, mids, tables, put):
    first_ref, twiddle_ref, second_ref = tables
    for c in range(SUB):
        first = jnp.dot(lhs[c], first_ref[...], preferred_element_type=jnp.float32)
        real, imag = first[:, :RADIX], first[:, RADIX:]
        turn_real, turn_imag = twiddle_ref[0], twiddle_ref[1]
        lanes = slice((c % 2) * RADIX, (c % 2 + 1) * RADIX)
        mids[c // 2, :RADIX, lanes] = (real * turn_real - imag * turn_imag).astype(jnp.bfloat16)
        mids[c // 2, RADIX:, lanes] = (real * turn_imag + imag * turn_real).astype(jnp.bfloat16)
    for i in range(SUB // 2):
        spectrum = jnp.dot(second_ref[...], mids[i], preferred_element_type=jnp.float32)
        real, imag = spectrum[:OUT], spectrum[OUT:]
        power = real * real + imag * imag
        put(2 * i, power[:, :RADIX])
        put(2 * i + 1, power[:, RADIX:])


def own_kernel(where, own, mask, window, out, wide, sums):
    def block(n, _):
        for half in range(2):
            stage(wide.at[half], sums.at[half], own.at[n], half)
        piece = (wide.at[0], wide.at[1], sums.at[0], sums.at[1], mask.at[n, 0])
        for c in range(SUB):
            out[n, c] = shape(c, piece, window)
        return 0

    lax.fori_loop(0, own.shape[0], block, 0)


def local_kernel(
    where, ready, other, mask, first, twiddle, second, window, out, wide, sums, lhs, mids
):
    def block(n, _):
        for half in range(2):
            stage(wide.at[half], sums.at[half], other.at[n], half)
        piece = (wide.at[0], wide.at[1], sums.at[0], sums.at[1], mask.at[n, 0])
        for c in range(SUB):
            lhs[c, :, :RADIX] = ready[n, c]
            lhs[c, :, RADIX:] = shape(c, piece, window)

        def put(c, power):
            out[n, c] = power

        pair_power(lhs, mids, (first, twiddle, second), put)
        return 0

    lax.fori_loop(0, other.shape[0], block, 0)


def cross_kernel(
    groups, where, own, other, lower0, lower1, upper0, upper1, base, weight,
    first, twiddle, second, window, mirror, out,
    load, held, wide, sums, lhs, mids, total, plain, turned, sems, held_sem,
):
    core, chip, group = where[0], where[1], where[2]
    sub = out.shape[0]
    low = group < groups // 2
    high = jnp.logical_not(low)
    rounds = jnp.where(jnp.logical_and(high, chip == groups - 1), 2, 1)
    edge = jnp.where(low, group, group - groups // 2) * sub
    inside = (2 * group + core) * sub

    def copy(source, slot, k):
        return pltpu.make_async_copy(source, load.at[slot, k], sems.at[slot, k])

    def fetch(u):
        slot = u & 1
        n = u // rounds
        again = u - n * rounds == 1
        start = jnp.logical_not(again)
        for index, lo, hi, up, down in (
            (0, own, other, upper0, lower0),
            (1, other, own, upper1, lower1),
        ):
            here = core == index

            @pl.when(jnp.logical_and(here, start))
            def _():
                copy(lo.at[inside + n, pl.ds(HALF, HALF)], slot, 0).start()
                copy(hi.at[inside + n, pl.ds(0, HALF)], slot, 1).start()

            @pl.when(jnp.logical_and(jnp.logical_and(here, start), low))
            def _():
                copy(hi.at[inside + n, pl.ds(HALF, HALF)], slot, 2).start()
                copy(up.at[edge + n], slot, 3).start()

            @pl.when(jnp.logical_and(jnp.logical_and(here, start), high))
            def _():
                copy(down.at[edge + n], slot, 2).start()
                copy(lo.at[inside + n, pl.ds(0, HALF)], slot, 3).start()

            @pl.when(jnp.logical_and(here, again))
            def _():
                copy(hi.at[inside + n, pl.ds(HALF, HALF)], slot, 0).start()
                for k in range(1, 4):
                    copy(up.at[0], slot, k).start()

    held_copy = pltpu.make_async_copy(base.at[pl.ds(group * sub, sub)], held, held_sem)
    fetch(0)
    held_copy.start()
    units = sub * rounds
    lane = lax.broadcasted_iota(jnp.int32, (KBANDS, RADIX), 1)

    def unit(u, _):
        slot = u & 1
        n = u // rounds
        r = u - n * rounds
        again = r == 1

        @pl.when(u + 1 < units)
        def _():
            fetch(u + 1)

        for k in range(4):
            copy(upper0.at[0], slot, k).wait()

        @pl.when(u == 0)
        def _():
            held_copy.wait()

        @pl.when(r == 0)
        def _():
            total[...] = held[n]

        for k in range(4):
            stage(wide.at[k], sums.at[k], load.at[slot, k], 0)
        masks = (jnp.where(again, 3, 1), jnp.where(again, 5, jnp.where(low, 3, 4)))
        for c in range(SUB):
            for s in range(2):
                piece = (
                    wide.at[2 * s], wide.at[2 * s + 1], sums.at[2 * s], sums.at[2 * s + 1],
                    weight.at[n, masks[s]],
                )
                lhs[c, :, s * RADIX : (s + 1) * RADIX] = shape(c, piece, window)

        def put(c, power):
            total[c] = total[c] + power

        pair_power(lhs, mids, (first, twiddle, second), put)

        @pl.when(r == rounds - 1)
        def _():
            for c in range(SUB):
                rows = slice(c * KBANDS, (c + 1) * KBANDS)
                plain[rows, :] = total[c, :KBANDS]
                turned[rows, :] = jnp.where(
                    lane == 0,
                    total[c, KBANDS : 2 * KBANDS],
                    total[c, KBANDS + 1 : 2 * KBANDS + 1],
                )
            plain[SUB * KBANDS :, :] = jnp.sum(weight[n, :4], axis=0)
            turned[SUB * KBANDS :, :] = jnp.zeros((SUB, RADIX), jnp.float32)
            reverse = jnp.dot(
                turned[...].astype(jnp.bfloat16), mirror[...], preferred_element_type=jnp.float32
            )
            out[n] = (plain[...] + reverse).astype(out.dtype)

        return 0

    lax.fori_loop(0, units, unit, 0)


def finish_kernel(keep, *refs):
    *got, scale, out, total = refs
    value = keep[0]
    for piece in got:
        value = value + piece[0].astype(jnp.float32)
    total[...] = value
    inverse = 1.0 / jnp.maximum(total[SUB * KBANDS :, :], 1.0)
    for j in range(KBANDS):
        value = total[pl.ds(j, SUB, stride=KBANDS), :]
        out[:, j * RADIX : (j + 1) * RADIX] = value * scale[j : j + 1, :] * inverse


def whole(array):
    return pl.BlockSpec(array.shape, lambda *_: (0,) * array.ndim)


def per_device(samples, valid):
    first, twiddle, second, window, mirror, scale = make_tables()
    tables = (first, twiddle, second, window)
    channels = samples.shape[0]
    size = lax.axis_size("chan")
    chips = size // 2
    half = chips // 2
    place = lax.axis_index("chan")
    core, chip = place & 1, place >> 1
    sub = channels // (SUB * size)

    def send(value, perm):
        return lax.ppermute(value, "chan", perm)

    def tiled(value):
        return value.reshape(channels // SUB, SUB, RADIX, RADIX).transpose(0, 2, 1, 3)

    swap = [(i, i ^ 1) for i in range(size)]
    links = range(chips - 1)
    tiles = tiled(samples)
    groups = tiles.reshape(chips, 2, sub, RADIX, SUB, RADIX)
    edges = [
        lax.dynamic_slice(
            groups,
            (core * half, c, 0, core * HALF, 0, 0),
            (half, 1, sub, HALF, SUB, RADIX),
        ).reshape(half * sub, HALF, SUB, RADIX)
        for c in range(2)
    ]
    onward = [[(2 * z + 1, 2 * z + 2 + c) for z in links] for c in range(2)]
    back = [[(2 * z + 2, 2 * z + c) for z in links] for c in range(2)]
    lower = [send(edges[c], onward[c]) for c in range(2)]
    upper = [send(edges[c], back[c]) for c in range(2)]
    other = tiled(send(samples, swap))

    theirs = send(valid, swap)
    before = sum(send(valid, onward[c]) for c in range(2))

    def spread(mask):
        count = mask.shape[1]
        mask = mask.astype(jnp.float32).reshape(chips, 2, sub, SUB, count)
        mask = lax.dynamic_index_in_dim(mask, core, 1, False).reshape(chips * sub, SUB, count)
        shape = (chips * sub, count, SUB, RADIX)
        return jnp.broadcast_to(mask.transpose(0, 2, 1)[..., None], shape)

    lo = jnp.where(core == 0, valid, theirs)
    hi = jnp.where(core == 0, theirs, valid)
    last = before[:, 1:]
    weight = spread(jnp.concatenate([lo, hi, last, jnp.zeros_like(last)], axis=1))

    step = 2 if sub % 2 == 0 else 1
    tile = (step, RADIX, SUB, RADIX)
    stripe = STEP * SUB
    half_wide = pltpu.VMEM((2, stripe, RADIX), jnp.float32)
    half_sums = pltpu.VMEM((2, SUB, RADIX), jnp.float32)
    lhs_shape = pltpu.VMEM((SUB, RADIX, 2 * RADIX), jnp.bfloat16)
    mids_shape = pltpu.VMEM((SUB // 2, 2 * RADIX, 2 * RADIX), jnp.bfloat16)
    local_grid = (chips, sub // step)

    def dense(g, i, w):
        return (g * (sub // step) + i, 0, 0, 0)

    def mine(g, i, w):
        return ((2 * g + w[0]) * (sub // step) + i, 0, 0, 0)

    def cost(parts):
        return pl.CostEstimate(
            flops=parts * 50_000 * samples.size // SEG * SEG // RADIX,
            transcendentals=0,
            bytes_accessed=parts * samples.size,
        )

    where = jnp.stack([core, chip]).astype(jnp.int32)
    ready = pl.pallas_call(
        own_kernel,
        grid_spec=pltpu.PrefetchScalarGridSpec(
            num_scalar_prefetch=1,
            grid=local_grid,
            in_specs=[
                pl.BlockSpec(tile, mine),
                pl.BlockSpec((step, 1, SUB, RADIX), dense),
                whole(window),
            ],
            out_specs=pl.BlockSpec((step, SUB, RADIX, RADIX), dense),
            scratch_shapes=[half_wide, half_sums],
        ),
        out_shape=jax.ShapeDtypeStruct((chips * sub, SUB, RADIX, RADIX), jnp.bfloat16),
        cost_estimate=cost(1),
        name="own_segments",
    )(where, tiles, spread(valid[:, :1]), window)
    partial = pl.pallas_call(
        local_kernel,
        grid_spec=pltpu.PrefetchScalarGridSpec(
            num_scalar_prefetch=1,
            grid=local_grid,
            in_specs=[
                pl.BlockSpec((step, SUB, RADIX, RADIX), dense),
                pl.BlockSpec(tile, mine),
                pl.BlockSpec((step, 1, SUB, RADIX), dense),
                *[whole(t) for t in tables],
            ],
            out_specs=pl.BlockSpec((step, SUB, OUT, RADIX), dense),
            scratch_shapes=[half_wide, half_sums, lhs_shape, mids_shape],
        ),
        out_shape=jax.ShapeDtypeStruct((chips * sub, SUB, OUT, RADIX), jnp.float32),
        cost_estimate=cost(3),
        name="local_segments",
    )(where, ready, other, spread(lax.optimization_barrier((theirs, ready))[0][:, :1]), *tables)

    anywhere = pl.BlockSpec(memory_space=pl.ANY)

    def cross(group, dtype):
        return pl.pallas_call(
            functools.partial(cross_kernel, chips),
            grid_spec=pltpu.PrefetchScalarGridSpec(
                num_scalar_prefetch=1,
                grid=(1,),
                in_specs=[
                    *[anywhere] * 7,
                    pl.BlockSpec((sub, SLOTS, SUB, RADIX), lambda i, w: (w[2], 0, 0, 0)),
                    *[whole(t) for t in tables],
                    whole(mirror),
                ],
                out_specs=pl.BlockSpec((sub, ROWS, RADIX), lambda i, w: (0, 0, 0)),
                scratch_shapes=[
                    pltpu.VMEM((2, 4, HALF, SUB, RADIX), jnp.bfloat16),
                    pltpu.VMEM((sub, SUB, OUT, RADIX), jnp.float32),
                    pltpu.VMEM((4, stripe, RADIX), jnp.float32),
                    pltpu.VMEM((4, SUB, RADIX), jnp.float32),
                    lhs_shape,
                    mids_shape,
                    pltpu.VMEM((SUB, OUT, RADIX), jnp.float32),
                    pltpu.VMEM((ROWS, RADIX), jnp.float32),
                    pltpu.VMEM((ROWS, RADIX), jnp.float32),
                    pltpu.SemaphoreType.DMA((2, 4)),
                    pltpu.SemaphoreType.DMA,
                ],
            ),
            out_shape=jax.ShapeDtypeStruct((sub, ROWS, RADIX), dtype),
        )(
            jnp.stack([core, chip, group]).astype(jnp.int32),
            tiles, other, *lower, *upper, partial, weight, *tables, mirror,
        )

    got, after = [], ready
    for shift in sorted(range(1, chips), key=lambda r: -min(r, chips - r)):
        target = (chip + shift) % chips
        target, _ = lax.optimization_barrier((target, after))
        away = cross(target, jnp.bfloat16)
        after = away
        around = [(i, (i + 2 * shift) % size) for i in range(size)]
        got.append(send(away, around))
    chip_last, _ = lax.optimization_barrier((chip, after))
    keep = cross(chip_last, jnp.float32)

    piece = pl.BlockSpec((1, ROWS, RADIX), lambda i: (i, 0, 0))
    return pl.pallas_call(
        finish_kernel,
        grid=(sub,),
        in_specs=[piece] * chips + [whole(scale)],
        out_specs=pl.BlockSpec((SUB, KBANDS * RADIX), lambda i: (i, 0)),
        out_shape=jax.ShapeDtypeStruct((sub * SUB, KBANDS * RADIX), jnp.float32),
        scratch_shapes=[pltpu.VMEM((ROWS, RADIX), jnp.float32)],
        name="finish",
    )(keep, *got, scale)


def solution(mesh):
    return jax.shard_map(
        per_device,
        mesh=mesh,
        in_specs=(P("tm", "chan"), P("tm", "chan")),
        out_specs=P(("tm", "chan"), None),
        check_vma=False,
    )
```

profile of v0, /device:TPU:0, one launch (start us, length us, event | category | flops | bytes accessed | tf_op | source)
XLA Modules:
  0.0 106.9 jit_solution(10206523789103650228)
XLA Ops:
  0.0 0.5 collective-permute-start
  0.5 3.1 %constant_dynamic-slice_fusion.1 = (bf16[2,1,4,64,8,128]{5,4,3,2,1,0:T(8,128)(2,1)}, bf16[2,1,4,64,8,128]{5,4,3,2,1,0:T(8,128)(2,1)}) fusion(bf16[4,2,4,128,8,128]{5,4,3,2,1,0:T(8,128)(2,1)} %bitcast.34, s32[]{:T(128)S(6)} %select_n.46, s32[]{:T(128)S(6)} %select_n.47), kind=kLoop, calls=%fused_computation.10 | loop fusion | bytes 4194312 | tf_op jit(solution)/shard_map/dynamic_slice | solution.py:270
  3.6 0.7 collective-permute-start.1
  4.3 1.3 %collective-permute-start.3 = (bf16[8,64,8,128]{3,2,1,0:T(8,128)(2,1)}, bf16[8,64,8,128]{3,2,1,0:T(8,128)(2,1)S(1)}, u32[]{:S(2)}, u32[]{:S(2)}) collective-permute-start(bf16[8,64,8,128]{3,2,1,0:T(8,128)(2,1)} %bitcast.10), channel_id=1, source_target_pairs={{2,0},{4,2},{6,4},{10,8},{12,10},{14,12},{18,16},{20,18},{22,20},{... | collective-permute-start | bytes 3145736 | tf_op jit(solution)/shard_map/ppermute | solution.py:260
  5.6 3.4 %collective-permute-start.5 = (s32[256,2]{0,1:T(2,128)}, s32[256,2]{0,1:T(2,128)S(1)}, u32[]{:S(2)}, u32[]{:S(2)}) collective-permute-start(s32[256,2]{0,1:T(2,128)} %param.9), channel_id=1, source_target_pairs={{0,1},{1,0},{2,3},{3,2},{4,5},{5,4},{6,7},{7,6},{8,9},{9,8},{10,11... | collective-permute-start | bytes 6152 | tf_op jit(solution)/shard_map/ppermute | solution.py:260
  9.0 0.6 collective-permute-start.6
  9.7 0.7 convert_reduce_fusion.1
  10.5 0.6 pad_add_fusion.where
  11.1 0.7 broadcast_in_dim.24.mask
  11.8 9.1 %own_segments.1.ready = bf16[16,8,128,128]{3,2,1,0:T(8,128)(2,1)} custom-call(s32[2]{0:T(128)} %pad_add_fusion.where, bf16[32,128,8,128]{3,2,1,0:T(8,128)(2,1)} %bitcast.35, f32[16,1,8,128]{3,2,1,0:T(8,128)} %broadcast_in_dim.24.mask, f32[128,128]{1,0:T(8,128)} %constant.61.clone.window), custom_call_target="tpu_custom_call" | custom-call | flops 1638400000 | bytes 4194304 | tf_op jit(solution)/shard_map/own_segments/pallas_call | solution.py:321
  20.9 0.6 pad_add_fusion.1
  21.6 0.7 collective-permute-start.7
  22.4 0.7 collective-permute-start.2
  23.1 1.7 %collective-permute-start.4 = (bf16[8,64,8,128]{3,2,1,0:T(8,128)(2,1)}, bf16[8,64,8,128]{3,2,1,0:T(8,128)(2,1)}, u32[]{:S(2)}, u32[]{:S(2)}) collective-permute-start(bf16[8,64,8,128]{3,2,1,0:T(8,128)(2,1)} %bitcast.41), channel_id=1, source_target_pairs={{2,1},{4,3},{6,5},{10,9},{12,11},{14,13},{18,17},{20,19},{22,21},{... | collective-permute-start | bytes 3145736 | tf_op jit(solution)/shard_map/ppermute | solution.py:260
  25.3 0.7 broadcast_in_dim.26.mask
  26.0 14.9 %local_segments.1.base = f32[16,8,72,128]{3,2,1,0:T(8,128)} custom-call(s32[2]{0:T(128)} %pad_add_fusion.where, bf16[16,8,128,128]{3,2,1,0:T(8,128)(2,1)} %own_segments.1.ready, bf16[32,128,8,128]{3,2,1,0:T(8,128)(2,1)} %bitcast.7.other, f32[16,1,8,128]{3,2,1,0:T(8,128)} %broadcast_in_dim.26.mask, bf16[256,256]{1,0:T(8,128)(2,1)} %constant.58.clone.first, ...), custom_call_target="tpu_custom_call" | custom-call | flops 4915200000 | bytes 12582912 | tf_op jit(solution)/shard_map/local_segments/pallas_call | solution.py:338
  41.0 1.1 %broadcast_in_dim.28.weight = f32[16,6,8,128]{3,2,1,0:T(8,128)} broadcast(f32[16,6,8]{2,1,0:T(8,128)S(1)} %bitcast.42), dimensions={0,1,2} | broadcast | bytes 396288 | tf_op jit(solution)/shard_map/broadcast_in_dim | solution.py:291
  42.0 0.3 copy-done.2
  42.3 0.3 copy-done.1
  42.7 8.1 %shard_map.82 = bf16[4,272,128]{2,1,0:T(8,128)(2,1)} custom-call(s32[3]{0:T(128)} %get-tuple-element.15.where, bf16[32,128,8,128]{3,2,1,0:T(8,128)(2,1)} %bitcast.36, bf16[32,128,8,128]{3,2,1,0:T(8,128)(2,1)} %bitcast.7.other, bf16[8,64,8,128]{3,2,1,0:T(8,128)(2,1)} %copy-done, bf16[8,64,8,128]{3,2,1,0:T(8,128)(2,1)} %copy-done.2, ...), custom_call_target="tpu_custom_call" | custom-call | tf_op jit(solution)/shard_map/pallas_call | solution.py:360
  50.8 0.6 pad_add_fusion.2.where
  51.4 8.1 %shard_map.83 = bf16[4,272,128]{2,1,0:T(8,128)(2,1)} custom-call(s32[3]{0:T(128)} %pad_add_fusion.2.where, bf16[32,128,8,128]{3,2,1,0:T(8,128)(2,1)} %bitcast.37, bf16[32,128,8,128]{3,2,1,0:T(8,128)(2,1)} %bitcast.7.other, bf16[8,64,8,128]{3,2,1,0:T(8,128)(2,1)} %copy-done, bf16[8,64,8,128]{3,2,1,0:T(8,128)(2,1)} %copy-done.2, ...), custom_call_target="tpu_custom_call" | custom-call | tf_op jit(solution)/shard_map/pallas_call | solution.py:360
  59.5 0.7 pad_add_fusion.3.where
  60.1 8.2 %shard_map.84 = bf16[4,272,128]{2,1,0:T(8,128)(2,1)} custom-call(s32[3]{0:T(128)} %pad_add_fusion.3.where, bf16[32,128,8,128]{3,2,1,0:T(8,128)(2,1)} %bitcast.38, bf16[32,128,8,128]{3,2,1,0:T(8,128)(2,1)} %bitcast.7.other, bf16[8,64,8,128]{3,2,1,0:T(8,128)(2,1)} %copy-done, bf16[8,64,8,128]{3,2,1,0:T(8,128)(2,1)} %copy-done.2, ...), custom_call_target="tpu_custom_call" | custom-call | tf_op jit(solution)/shard_map/pallas_call | solution.py:360
  68.3 14.0 %collective-permute-start.10 = (bf16[4,272,128]{2,1,0:T(8,128)(2,1)}, bf16[4,272,128]{2,1,0:T(8,128)(2,1)S(1)}, u32[]{:S(2)}, u32[]{:S(2)}) collective-permute-start(bf16[4,272,128]{2,1,0:T(8,128)(2,1)} %shard_map.84), channel_id=1, source_target_pairs={{0,6},{1,7},{2,0},{3,1},{4,2},{5,3},{6,4},{7,5},{8,14},{9,15},{10,... | collective-permute-start | bytes 835592 | tf_op jit(solution)/shard_map/ppermute | solution.py:260
  82.3 0.6 collective-permute-start.8
  82.9 0.7 pad_add_fusion.4.where
  83.6 8.2 %shard_map.85.keep = f32[4,272,128]{2,1,0:T(8,128)} custom-call(s32[3]{0:T(128)} %pad_add_fusion.4.where, bf16[32,128,8,128]{3,2,1,0:T(8,128)(2,1)} %bitcast.39, bf16[32,128,8,128]{3,2,1,0:T(8,128)(2,1)} %bitcast.7.other, bf16[8,64,8,128]{3,2,1,0:T(8,128)(2,1)} %copy-done, bf16[8,64,8,128]{3,2,1,0:T(8,128)(2,1)} %copy-done.2, ...), custom_call_target="tpu_custom_call" | custom-call | tf_op jit(solution)/shard_map/pallas_call | solution.py:360
  91.8 4.0 %collective-permute-done.9.refs_1_ = bf16[4,272,128]{2,1,0:T(8,128)(2,1)S(1)} collective-permute-done((bf16[4,272,128]{2,1,0:T(8,128)(2,1)S(1)}, bf16[4,272,128]{2,1,0:T(8,128)(2,1)S(1)}, u32[]{:S(2)}, u32[]{:S(2)}) %collective-permute-start.9) | collective-permute-done | bytes 278560 | tf_op jit(solution)/shard_map/ppermute | solution.py:260
  95.8 6.9 %collective-permute-done.8.refs_0_ = bf16[4,272,128]{2,1,0:T(8,128)(2,1)S(1)} collective-permute-done((bf16[4,272,128]{2,1,0:T(8,128)(2,1)S(1)}, bf16[4,272,128]{2,1,0:T(8,128)(2,1)S(1)}, u32[]{:S(2)}, u32[]{:S(2)}) %collective-permute-start.8) | collective-permute-done | bytes 278560 | tf_op jit(solution)/shard_map/ppermute | solution.py:260
  102.8 0.7 copy-done.7
  103.5 3.5 %finish.1 = f32[32,4224]{1,0:T(8,128)} custom-call(f32[4,272,128]{2,1,0:T(8,128)} %shard_map.85.keep, bf16[4,272,128]{2,1,0:T(8,128)(2,1)} %copy-done.7, bf16[4,272,128]{2,1,0:T(8,128)(2,1)} %copy-done.6, bf16[4,272,128]{2,1,0:T(8,128)(2,1)} %copy-done.5, f32[33,128]{1,0:T(8,128)} %constant.63.clone.refs_3_), custom_call_target="tpu_custom_call" | custom-call | tf_op jit(solution)/shard_map/finish/pallas_call | solution.py:404
  (38 shorter events, 0.8 us)
Async XLA Ops:
  0.0 25.3 %collective-permute-start = (bf16[256,16384]{1,0:T(8,128)(2,1)}, bf16[256,16384]{1,0:T(8,128)(2,1)}, u32[]{:S(2)}, u32[]{:S(2)}) collective-permute-start(bf16[256,16384]{1,0:T(8,128)(2,1)} %param.8), channel_id=1, source_target_pairs={{0,1},{1,0},{2,3},{3,2},{4,5},{5,4},{6,7},{7,6},{8,9},{9,8},{10,11... | collective-permute-start | bytes 25165832 | tf_op jit(solution)/shard_map/ppermute | solution.py:260
  0.5 21.1 %copy-start.8 = (s32[256,2]{0,1:T(2,128)S(1)}, s32[256,2]{0,1:T(2,128)}, u32[]{:S(2)}) copy-start(s32[256,2]{0,1:T(2,128)} %param.9) | copy-start | bytes 6148
  3.6 37.3 %collective-permute-start.1 = (bf16[8,64,8,128]{3,2,1,0:T(8,128)(2,1)}, bf16[8,64,8,128]{3,2,1,0:T(8,128)(2,1)S(1)}, u32[]{:S(2)}, u32[]{:S(2)}) collective-permute-start(bf16[8,64,8,128]{3,2,1,0:T(8,128)(2,1)} %bitcast.10), channel_id=1, source_target_pairs={{1,2},{3,4},{5,6},{9,10},{11,12},{13,14},{17,18},{19,20},{21,22},{... | collective-permute-start | bytes 3145736 | tf_op jit(solution)/shard_map/ppermute | solution.py:260
  4.3 36.6 %collective-permute-start.3 = (bf16[8,64,8,128]{3,2,1,0:T(8,128)(2,1)}, bf16[8,64,8,128]{3,2,1,0:T(8,128)(2,1)S(1)}, u32[]{:S(2)}, u32[]{:S(2)}) collective-permute-start(bf16[8,64,8,128]{3,2,1,0:T(8,128)(2,1)} %bitcast.10), channel_id=1, source_target_pairs={{2,0},{4,2},{6,4},{10,8},{12,10},{14,12},{18,16},{20,18},{22,20},{... | collective-permute-start | bytes 3145736 | tf_op jit(solution)/shard_map/ppermute | solution.py:260
  5.6 16.0 %collective-permute-start.5 = (s32[256,2]{0,1:T(2,128)}, s32[256,2]{0,1:T(2,128)S(1)}, u32[]{:S(2)}, u32[]{:S(2)}) collective-permute-start(s32[256,2]{0,1:T(2,128)} %param.9), channel_id=1, source_target_pairs={{0,1},{1,0},{2,3},{3,2},{4,5},{5,4},{6,7},{7,6},{8,9},{9,8},{10,11... | collective-permute-start | bytes 6152 | tf_op jit(solution)/shard_map/ppermute | solution.py:260
  9.0 13.4 %collective-permute-start.6 = (s32[256,2]{0,1:T(2,128)}, s32[256,2]{0,1:T(2,128)S(1)}, u32[]{:S(2)}, u32[]{:S(2)}) collective-permute-start(s32[256,2]{0,1:T(2,128)} %param.9), channel_id=1, source_target_pairs={{1,2},{3,4},{5,6},{9,10},{11,12},{13,14},{17,18},{19,20},{21,22},{... | collective-permute-start | bytes 6152 | tf_op jit(solution)/shard_map/ppermute | solution.py:260
  21.6 1.5 %collective-permute-start.7 = (s32[256,2]{0,1:T(2,128)S(1)}, s32[256,2]{0,1:T(2,128)S(1)}, u32[]{:S(2)}, u32[]{:S(2)}) collective-permute-start(s32[256,2]{0,1:T(2,128)S(1)} %copy-done.8), channel_id=1, source_target_pairs={{1,3},{3,5},{5,7},{9,11},{11,13},{13,15},{17,19},{19,21},{21,23},{... | collective-permute-start | bytes 6152 | tf_op jit(solution)/shard_map/ppermute | solution.py:260
  22.4 18.5 %collective-permute-start.2 = (bf16[8,64,8,128]{3,2,1,0:T(8,128)(2,1)}, bf16[8,64,8,128]{3,2,1,0:T(8,128)(2,1)S(1)}, u32[]{:S(2)}, u32[]{:S(2)}) collective-permute-start(bf16[8,64,8,128]{3,2,1,0:T(8,128)(2,1)} %bitcast.40), channel_id=1, source_target_pairs={{1,3},{3,5},{5,7},{9,11},{11,13},{13,15},{17,19},{19,21},{21,23},{... | collective-permute-start | bytes 3145736 | tf_op jit(solution)/shard_map/ppermute | solution.py:260
  23.1 17.8 %collective-permute-start.4 = (bf16[8,64,8,128]{3,2,1,0:T(8,128)(2,1)}, bf16[8,64,8,128]{3,2,1,0:T(8,128)(2,1)}, u32[]{:S(2)}, u32[]{:S(2)}) collective-permute-start(bf16[8,64,8,128]{3,2,1,0:T(8,128)(2,1)} %bitcast.41), channel_id=1, source_target_pairs={{2,1},{4,3},{6,5},{10,9},{12,11},{14,13},{18,17},{20,19},{22,21},{... | collective-permute-start | bytes 3145736 | tf_op jit(solution)/shard_map/ppermute | solution.py:260
  40.9 1.1 %copy-start = (bf16[8,64,8,128]{3,2,1,0:T(8,128)(2,1)}, bf16[8,64,8,128]{3,2,1,0:T(8,128)(2,1)S(1)}, u32[]{:S(2)}) copy-start(bf16[8,64,8,128]{3,2,1,0:T(8,128)(2,1)S(1)} %collective-permute-done.1.lower0) | copy-start | bytes 3145732
  40.9 1.4 %copy-start.2 = (bf16[8,64,8,128]{3,2,1,0:T(8,128)(2,1)}, bf16[8,64,8,128]{3,2,1,0:T(8,128)(2,1)S(1)}, u32[]{:S(2)}) copy-start(bf16[8,64,8,128]{3,2,1,0:T(8,128)(2,1)S(1)} %collective-permute-done.2.lower1) | copy-start | bytes 3145732
  40.9 1.7 %copy-start.1 = (bf16[8,64,8,128]{3,2,1,0:T(8,128)(2,1)}, bf16[8,64,8,128]{3,2,1,0:T(8,128)(2,1)S(1)}, u32[]{:S(2)}) copy-start(bf16[8,64,8,128]{3,2,1,0:T(8,128)(2,1)S(1)} %collective-permute-done.3.upper0) | copy-start | bytes 3145732
  60.1 22.2 %copy-start.4 = (bf16[4,272,128]{2,1,0:T(8,128)(2,1)S(1)}, bf16[4,272,128]{2,1,0:T(8,128)(2,1)}, u32[]{:S(2)}) copy-start(bf16[4,272,128]{2,1,0:T(8,128)(2,1)} %shard_map.83) | copy-start | bytes 835588
  60.1 22.2 %copy-start.3 = (bf16[4,272,128]{2,1,0:T(8,128)(2,1)S(1)}, bf16[4,272,128]{2,1,0:T(8,128)(2,1)}, u32[]{:S(2)}) copy-start(bf16[4,272,128]{2,1,0:T(8,128)(2,1)} %shard_map.82) | copy-start | bytes 835588
  68.3 23.5 %collective-permute-start.10 = (bf16[4,272,128]{2,1,0:T(8,128)(2,1)}, bf16[4,272,128]{2,1,0:T(8,128)(2,1)S(1)}, u32[]{:S(2)}, u32[]{:S(2)}) collective-permute-start(bf16[4,272,128]{2,1,0:T(8,128)(2,1)} %shard_map.84), channel_id=1, source_target_pairs={{0,6},{1,7},{2,0},{3,1},{4,2},{5,3},{6,4},{7,5},{8,14},{9,15},{10,... | collective-permute-start | bytes 835592 | tf_op jit(solution)/shard_map/ppermute | solution.py:260
  82.3 13.5 %collective-permute-start.9 = (bf16[4,272,128]{2,1,0:T(8,128)(2,1)S(1)}, bf16[4,272,128]{2,1,0:T(8,128)(2,1)S(1)}, u32[]{:S(2)}, u32[]{:S(2)}) collective-permute-start(bf16[4,272,128]{2,1,0:T(8,128)(2,1)S(1)} %copy-done.4), channel_id=1, source_target_pairs={{0,2},{1,3},{2,4},{3,5},{4,6},{5,7},{6,0},{7,1},{8,10},{9,11},{10,... | collective-permute-start | bytes 835592 | tf_op jit(solution)/shard_map/ppermute | solution.py:260
  82.3 20.4 %collective-permute-start.8 = (bf16[4,272,128]{2,1,0:T(8,128)(2,1)S(1)}, bf16[4,272,128]{2,1,0:T(8,128)(2,1)S(1)}, u32[]{:S(2)}, u32[]{:S(2)}) collective-permute-start(bf16[4,272,128]{2,1,0:T(8,128)(2,1)S(1)} %copy-done.3), channel_id=1, source_target_pairs={{0,4},{1,5},{2,6},{3,7},{4,0},{5,1},{6,2},{7,3},{8,12},{9,13},{10,... | collective-permute-start | bytes 835592 | tf_op jit(solution)/shard_map/ppermute | solution.py:260
  91.8 10.9 %copy-start.5 = (bf16[4,272,128]{2,1,0:T(8,128)(2,1)}, bf16[4,272,128]{2,1,0:T(8,128)(2,1)S(1)}, u32[]{:S(2)}) copy-start(bf16[4,272,128]{2,1,0:T(8,128)(2,1)S(1)} %collective-permute-done.10.refs_2_) | copy-start | bytes 835588
  95.8 6.9 %copy-start.6 = (bf16[4,272,128]{2,1,0:T(8,128)(2,1)}, bf16[4,272,128]{2,1,0:T(8,128)(2,1)S(1)}, u32[]{:S(2)}) copy-start(bf16[4,272,128]{2,1,0:T(8,128)(2,1)S(1)} %collective-permute-done.9.refs_1_) | copy-start | bytes 835588
  102.8 0.7 copy-start.7
where the time goes:
time: 108 us; the launch traced here: 107 us
  Pallas kernels  60 us (56%)
  starting transfers between devices  24.2 us (22%)
  waiting for transfers between devices  10.9 us (10%)
  local copies, waits for them, and re-layouts  7.54 us (7%)
  other arithmetic  4 us (4%)
    pallas_call x4, Pallas kernels, cross(): pl.pallas_call(functools.partial(cross_kernel, chips), grid_spec=pltpu.Pr...  32.6 us
    ppermute x11, starting transfers between devices, send(): return lax.ppermute(value, 'chan', perm)  24.2 us
    pallas_call x1, Pallas kernels, per_device(): pl.pallas_call(local_kernel, grid_spec=pltpu.PrefetchScalarGridSpec(num_s...  14.9 us
    ppermute x11, waiting for transfers between devices, send(): return lax.ppermute(value, 'chan', perm)  10.9 us
    pallas_call x1, Pallas kernels, per_device(): pl.pallas_call(own_kernel, grid_spec=pltpu.PrefetchScalarGridSpec(num_sca...  9.07 us
    pallas_call x1, Pallas kernels, per_device(): pl.pallas_call(finish_kernel, grid=(sub,), in_specs=[piece] * chips + [wh...  3.48 us
    dynamic_slice x1, local copies, waits for them, and re-layouts, per_device(): lax.dynamic_slice(groups, (core * half, c, 0, core * HALF, 0, 0), (half,...  3.09 us
    another operation x4, other arithmetic, cross(): jnp.stack([core, chip, group]).astype(jnp.int32)  2.56 us
  transfers between devices with their start and end apart: 11, of which 2 were waited for; matrix products, arithmetic and copies ran while one was open for 7% of the time, Pallas kernels for 30%

commit v1 on v0

--- a/solution.py
+++ b/solution.py
@@ -17,7 +17,6 @@
 OUT = 72
 ROWS = SUB * KBANDS + SUB
 SEG = RADIX * RADIX
-SLOTS = 6
 
 
 def make_tables():
@@ -84,28 +83,20 @@
         put(2 * i + 1, power[:, RADIX:])
 
 
-def own_kernel(where, own, mask, window, out, wide, sums):
+def local_kernel(
+    where, own, other, mask, first, twiddle, second, window, out, wide, sums, lhs, mids
+):
     def block(n, _):
         for half in range(2):
             stage(wide.at[half], sums.at[half], own.at[n], half)
-        piece = (wide.at[0], wide.at[1], sums.at[0], sums.at[1], mask.at[n, 0])
+            stage(wide.at[2 + half], sums.at[2 + half], other.at[n], half)
         for c in range(SUB):
-            out[n, c] = shape(c, piece, window)
-        return 0
-
-    lax.fori_loop(0, own.shape[0], block, 0)
-
-
-def local_kernel(
-    where, ready, other, mask, first, twiddle, second, window, out, wide, sums, lhs, mids
-):
-    def block(n, _):
-        for half in range(2):
-            stage(wide.at[half], sums.at[half], other.at[n], half)
-        piece = (wide.at[0], wide.at[1], sums.at[0], sums.at[1], mask.at[n, 0])
-        for c in range(SUB):
-            lhs[c, :, :RADIX] = ready[n, c]
-            lhs[c, :, RADIX:] = shape(c, piece, window)
+            for s in range(2):
+                piece = (
+                    wide.at[2 * s], wide.at[2 * s + 1], sums.at[2 * s], sums.at[2 * s + 1],
+                    mask.at[n, s],
+                )
+                lhs[c, :, s * RADIX : (s + 1) * RADIX] = shape(c, piece, window)
 
         def put(c, power):
             out[n, c] = power
@@ -113,30 +104,50 @@
         pair_power(lhs, mids, (first, twiddle, second), put)
         return 0
 
-    lax.fori_loop(0, other.shape[0], block, 0)
+    lax.fori_loop(0, own.shape[0], block, 0)
 
 
 def cross_kernel(
-    groups, where, own, other, lower0, lower1, upper0, upper1, base, weight,
-    first, twiddle, second, window, mirror, out,
-    load, held, wide, sums, lhs, mids, total, plain, turned, sems, held_sem,
+    groups, sub, count, where, own, other, lower0, lower1, upper0, upper1, base, weight,
+    first, twiddle, second, window, mirror, *rest,
 ):
-    core, chip, group = where[0], where[1], where[2]
-    sub = out.shape[0]
-    low = group < groups // 2
-    high = jnp.logical_not(low)
-    rounds = jnp.where(jnp.logical_and(high, chip == groups - 1), 2, 1)
-    edge = jnp.where(low, group, group - groups // 2) * sub
-    inside = (2 * group + core) * sub
+    outs = rest[:count]
+    load, held, wide, sums, lhs, mids, total, plain, turned, sems, held_sems = rest[count:]
+    core, chip = where[0], where[1]
+
+    def facts(i):
+        group = where[2 + i]
+        low = group < groups // 2
+        last = jnp.logical_and(jnp.logical_not(low), chip == groups - 1)
+        return group, low, jnp.where(last, 2, 1)
+
+    starts = [jnp.int32(0)]
+    for i in range(count):
+        starts.append(starts[-1] + sub * facts(i)[2])
+    units = starts[-1]
+
+    def find(u):
+        index = jnp.int32(0)
+        start = jnp.int32(0)
+        for i in range(1, count):
+            index = jnp.where(u >= starts[i], i, index)
+            start = jnp.where(u >= starts[i], starts[i], start)
+        group, low, rounds = facts(index)
+        n = (u - start) >> (rounds - 1)
+        again = jnp.logical_and(rounds == 2, ((u - start) & 1) == 1)
+        final = jnp.logical_or(rounds == 1, again)
+        return index, group, low, n, again, final
 
     def copy(source, slot, k):
         return pltpu.make_async_copy(source, load.at[slot, k], sems.at[slot, k])
 
     def fetch(u):
         slot = u & 1
-        n = u // rounds
-        again = u - n * rounds == 1
+        _, group, low, n, again, _ = find(u)
         start = jnp.logical_not(again)
+        high = jnp.logical_not(low)
+        edge = jnp.where(low, group, group - groups // 2) * sub
+        inside = (2 * group + core) * sub
         for index, lo, hi, up, down in (
             (0, own, other, upper0, lower0),
             (1, other, own, upper1, lower1),
@@ -164,17 +175,18 @@
                 for k in range(1, 4):
                     copy(up.at[0], slot, k).start()
 
-    held_copy = pltpu.make_async_copy(base.at[pl.ds(group * sub, sub)], held, held_sem)
+    held_copies = [
+        pltpu.make_async_copy(base.at[pl.ds(where[2 + i] * sub, sub)], held.at[i], held_sems.at[i])
+        for i in range(count)
+    ]
     fetch(0)
-    held_copy.start()
-    units = sub * rounds
+    for held_copy in held_copies:
+        held_copy.start()
     lane = lax.broadcasted_iota(jnp.int32, (KBANDS, RADIX), 1)
 
     def unit(u, _):
         slot = u & 1
-        n = u // rounds
-        r = u - n * rounds
-        again = r == 1
+        index, group, low, n, again, final = find(u)
 
         @pl.when(u + 1 < units)
         def _():
@@ -185,12 +197,14 @@
 
         @pl.when(u == 0)
         def _():
-            held_copy.wait()
-
-        @pl.when(r == 0)
+            for held_copy in held_copies:
+                held_copy.wait()
+
+        @pl.when(jnp.logical_not(again))
         def _():
-            total[...] = held[n]
-
+            total[...] = held[index, n]
+
+        row = group * sub + n
         for k in range(4):
             stage(wide.at[k], sums.at[k], load.at[slot, k], 0)
         masks = (jnp.where(again, 3, 1), jnp.where(again, 5, jnp.where(low, 3, 4)))
@@ -198,7 +212,7 @@
             for s in range(2):
                 piece = (
                     wide.at[2 * s], wide.at[2 * s + 1], sums.at[2 * s], sums.at[2 * s + 1],
-                    weight.at[n, masks[s]],
+                    weight.at[row, masks[s]],
                 )
                 lhs[c, :, s * RADIX : (s + 1) * RADIX] = shape(c, piece, window)
 
@@ -207,7 +221,7 @@
 
         pair_power(lhs, mids, (first, twiddle, second), put)
 
-        @pl.when(r == rounds - 1)
+        @pl.when(final)
         def _():
             for c in range(SUB):
                 rows = slice(c * KBANDS, (c + 1) * KBANDS)
@@ -217,28 +231,36 @@
                     total[c, KBANDS : 2 * KBANDS],
                     total[c, KBANDS + 1 : 2 * KBANDS + 1],
                 )
-            plain[SUB * KBANDS :, :] = jnp.sum(weight[n, :4], axis=0)
+            plain[SUB * KBANDS :, :] = jnp.sum(weight[row, :4], axis=0)
             turned[SUB * KBANDS :, :] = jnp.zeros((SUB, RADIX), jnp.float32)
             reverse = jnp.dot(
                 turned[...].astype(jnp.bfloat16), mirror[...], preferred_element_type=jnp.float32
             )
-            out[n] = (plain[...] + reverse).astype(out.dtype)
+            packed = (plain[...] + reverse).astype(jnp.bfloat16)
+            for i, out in enumerate(outs):
+
+                @pl.when(index == i)
+                def _():
+                    out[n] = packed
 
         return 0
 
     lax.fori_loop(0, units, unit, 0)
 
 
-def finish_kernel(keep, *refs):
-    *got, scale, out, total = refs
-    value = keep[0]
-    for piece in got:
-        value = value + piece[0].astype(jnp.float32)
-    total[...] = value
-    inverse = 1.0 / jnp.maximum(total[SUB * KBANDS :, :], 1.0)
-    for j in range(KBANDS):
-        value = total[pl.ds(j, SUB, stride=KBANDS), :]
-        out[:, j * RADIX : (j + 1) * RADIX] = value * scale[j : j + 1, :] * inverse
+def finish_kernel(*refs):
+    *pieces, scale, out, total = refs
+    for n in range(out.shape[0] // SUB):
+        value = pieces[0][n].astype(jnp.float32)
+        for piece in pieces[1:]:
+            value = value + piece[n].astype(jnp.float32)
+        total[...] = value
+        inverse = 1.0 / jnp.maximum(total[SUB * KBANDS :, :], 1.0)
+        for j in range(KBANDS):
+            value = total[pl.ds(j, SUB, stride=KBANDS), :]
+            out[n * SUB : (n + 1) * SUB, j * RADIX : (j + 1) * RADIX] = (
+                value * scale[j : j + 1, :] * inverse
+            )
 
 
 def whole(array):
@@ -298,8 +320,8 @@
     step = 2 if sub % 2 == 0 else 1
     tile = (step, RADIX, SUB, RADIX)
     stripe = STEP * SUB
-    half_wide = pltpu.VMEM((2, stripe, RADIX), jnp.float32)
-    half_sums = pltpu.VMEM((2, SUB, RADIX), jnp.float32)
+    wide_shape = pltpu.VMEM((4, stripe, RADIX), jnp.float32)
+    sums_shape = pltpu.VMEM((4, SUB, RADIX), jnp.float32)
     lhs_shape = pltpu.VMEM((SUB, RADIX, 2 * RADIX), jnp.bfloat16)
     mids_shape = pltpu.VMEM((SUB // 2, 2 * RADIX, 2 * RADIX), jnp.bfloat16)
     local_grid = (chips, sub // step)
@@ -310,106 +332,77 @@
     def mine(g, i, w):
         return ((2 * g + w[0]) * (sub // step) + i, 0, 0, 0)
 
-    def cost(parts):
-        return pl.CostEstimate(
-            flops=parts * 50_000 * samples.size // SEG * SEG // RADIX,
-            transcendentals=0,
-            bytes_accessed=parts * samples.size,
-        )
-
     where = jnp.stack([core, chip]).astype(jnp.int32)
-    ready = pl.pallas_call(
-        own_kernel,
-        grid_spec=pltpu.PrefetchScalarGridSpec(
-            num_scalar_prefetch=1,
-            grid=local_grid,
-            in_specs=[
-                pl.BlockSpec(tile, mine),
-                pl.BlockSpec((step, 1, SUB, RADIX), dense),
-                whole(window),
-            ],
-            out_specs=pl.BlockSpec((step, SUB, RADIX, RADIX), dense),
-            scratch_shapes=[half_wide, half_sums],
-        ),
-        out_shape=jax.ShapeDtypeStruct((chips * sub, SUB, RADIX, RADIX), jnp.bfloat16),
-        cost_estimate=cost(1),
-        name="own_segments",
-    )(where, tiles, spread(valid[:, :1]), window)
     partial = pl.pallas_call(
         local_kernel,
         grid_spec=pltpu.PrefetchScalarGridSpec(
             num_scalar_prefetch=1,
             grid=local_grid,
             in_specs=[
-                pl.BlockSpec((step, SUB, RADIX, RADIX), dense),
                 pl.BlockSpec(tile, mine),
-                pl.BlockSpec((step, 1, SUB, RADIX), dense),
+                pl.BlockSpec(tile, mine),
+                pl.BlockSpec((step, 2, SUB, RADIX), dense),
                 *[whole(t) for t in tables],
             ],
             out_specs=pl.BlockSpec((step, SUB, OUT, RADIX), dense),
-            scratch_shapes=[half_wide, half_sums, lhs_shape, mids_shape],
+            scratch_shapes=[wide_shape, sums_shape, lhs_shape, mids_shape],
         ),
         out_shape=jax.ShapeDtypeStruct((chips * sub, SUB, OUT, RADIX), jnp.float32),
-        cost_estimate=cost(3),
         name="local_segments",
-    )(where, ready, other, spread(lax.optimization_barrier((theirs, ready))[0][:, :1]), *tables)
+    )(where, tiles, other, spread(jnp.concatenate([valid[:, :1], theirs[:, :1]], axis=1)), *tables)
 
     anywhere = pl.BlockSpec(memory_space=pl.ANY)
 
-    def cross(group, dtype):
+    def cross(targets):
+        count = len(targets)
         return pl.pallas_call(
-            functools.partial(cross_kernel, chips),
+            functools.partial(cross_kernel, chips, sub, count),
             grid_spec=pltpu.PrefetchScalarGridSpec(
                 num_scalar_prefetch=1,
                 grid=(1,),
                 in_specs=[
                     *[anywhere] * 7,
-                    pl.BlockSpec((sub, SLOTS, SUB, RADIX), lambda i, w: (w[2], 0, 0, 0)),
+                    whole(weight),
                     *[whole(t) for t in tables],
                     whole(mirror),
                 ],
-                out_specs=pl.BlockSpec((sub, ROWS, RADIX), lambda i, w: (0, 0, 0)),
+                out_specs=[pl.BlockSpec((sub, ROWS, RADIX), lambda i, w: (0, 0, 0))] * count,
                 scratch_shapes=[
                     pltpu.VMEM((2, 4, HALF, SUB, RADIX), jnp.bfloat16),
-                    pltpu.VMEM((sub, SUB, OUT, RADIX), jnp.float32),
-                    pltpu.VMEM((4, stripe, RADIX), jnp.float32),
-                    pltpu.VMEM((4, SUB, RADIX), jnp.float32),
+                    pltpu.VMEM((count, sub, SUB, OUT, RADIX), jnp.float32),
+                    wide_shape,
+                    sums_shape,
                     lhs_shape,
                     mids_shape,
                     pltpu.VMEM((SUB, OUT, RADIX), jnp.float32),
                     pltpu.VMEM((ROWS, RADIX), jnp.float32),
                     pltpu.VMEM((ROWS, RADIX), jnp.float32),
                     pltpu.SemaphoreType.DMA((2, 4)),
-                    pltpu.SemaphoreType.DMA,
+                    pltpu.SemaphoreType.DMA((count,)),
                 ],
             ),
-            out_shape=jax.ShapeDtypeStruct((sub, ROWS, RADIX), dtype),
+            out_shape=[jax.ShapeDtypeStruct((sub, ROWS, RADIX), jnp.bfloat16)] * count,
         )(
-            jnp.stack([core, chip, group]).astype(jnp.int32),
+            jnp.stack([core, chip, *targets]).astype(jnp.int32),
             tiles, other, *lower, *upper, partial, weight, *tables, mirror,
         )
 
-    got, after = [], ready
-    for shift in sorted(range(1, chips), key=lambda r: -min(r, chips - r)):
-        target = (chip + shift) % chips
-        target, _ = lax.optimization_barrier((target, after))
-        away = cross(target, jnp.bfloat16)
-        after = away
+    shifts = sorted(range(1, chips), key=lambda r: (-min(r, chips - r), r)) + [0]
+    targets = [jnp.where(chip + r >= chips, chip + r - chips, chip + r) for r in shifts]
+    early = cross(targets[:half])
+    rest, _ = lax.optimization_barrier((jnp.stack(targets[half:]), early[-1]))
+    late = cross([rest[i] for i in range(chips - half)])
+    pieces = [*early, *late]
+    for k, shift in enumerate(shifts[:-1]):
         around = [(i, (i + 2 * shift) % size) for i in range(size)]
-        got.append(send(away, around))
-    chip_last, _ = lax.optimization_barrier((chip, after))
-    keep = cross(chip_last, jnp.float32)
-
-    piece = pl.BlockSpec((1, ROWS, RADIX), lambda i: (i, 0, 0))
+        pieces[k] = send(pieces[k], around)
+
     return pl.pallas_call(
         finish_kernel,
-        grid=(sub,),
-        in_specs=[piece] * chips + [whole(scale)],
-        out_specs=pl.BlockSpec((SUB, KBANDS * RADIX), lambda i: (i, 0)),
         out_shape=jax.ShapeDtypeStruct((sub * SUB, KBANDS * RADIX), jnp.float32),
         scratch_shapes=[pltpu.VMEM((ROWS, RADIX), jnp.float32)],
         name="finish",
-    )(keep, *got, scale)
+    )(*pieces, scale)
 
 
 def solution(mesh):

time: 108 us -> 108 us (level); the launches traced: 107 us -> 106 us
  Pallas kernels: 60 us -> 43.3 us
  waiting for transfers between devices: 10.9 us -> 27.6 us
  other arithmetic: 4 us -> 2.7 us
    pallas_call x6 -> x3, Pallas kernels: 45.1 us -> 27.9 us  [the longest x2 25.6 us: cross(): pl.pallas_call(functools.partial(cross_kernel, chips, sub, count), grid_s...]
    ppermute x11, waiting for transfers between devices: 10.9 us -> 27.6 us  [send(): return lax.ppermute(value, 'chan', perm)]
    another operation x4 -> x3, other arithmetic: 2.56 us -> 1.28 us  [the longest x2 1.21 us: cross(): jnp.stack([core, chip, *targets]).astype(jnp.int32)]
    broadcast_in_dim x3 -> x2, local copies, waits for them, and re-layouts: 2.51 us -> 1.86 us  [spread(): return jnp.broadcast_to(mask.transpose(0, 2, 1)[..., None], shape)]
  transfers between devices with their start and end apart: 11 -> 11, of which waited for: 2 -> 3; matrix products, arithmetic and copies ran while one was open for 7% -> 7% of each run, Pallas kernels for 30% -> 15%
where the time goes in v1:
time: 108 us; the launch traced here: 106 us
  Pallas kernels  43.3 us (40%)
  waiting for transfers between devices  27.6 us (26%)
  starting transfers between devices  24.3 us (22%)
  local copies, waits for them, and re-layouts  7.64 us (7%)
  other arithmetic  2.7 us (2%)
    ppermute x11, waiting for transfers between devices, send(): return lax.ppermute(value, 'chan', perm)  27.6 us
    pallas_call x2, Pallas kernels, cross(): pl.pallas_call(functools.partial(cross_kernel, chips, sub, count), grid_s...  25.6 us
    ppermute x11, starting transfers between devices, send(): return lax.ppermute(value, 'chan', perm)  24.3 us
    pallas_call x1, Pallas kernels, per_device(): pl.pallas_call(local_kernel, grid_spec=pltpu.PrefetchScalarGridSpec(num_s...  15.4 us
    dynamic_slice x1, local copies, waits for them, and re-layouts, per_device(): lax.dynamic_slice(groups, (core * half, c, 0, core * HALF, 0, 0), (half,...  3.06 us
    pallas_call x1, Pallas kernels, per_device(): pl.pallas_call(finish_kernel, out_shape=jax.ShapeDtypeStruct((sub * SUB,...  2.23 us
  transfers between devices with their start and end apart: 11, of which 3 were waited for; matrix products, arithmetic and copies ran while one was open for 7% of the time, Pallas kernels for 15%

profile of v1, /device:TPU:0, one launch (start us, length us, event | category | flops | bytes accessed | tf_op | source)
XLA Modules:
  0.0 105.8 jit_solution(3863459441893096470)
XLA Ops:
  0.0 0.5 collective-permute-start
  0.5 0.6 collective-permute-start.7
  1.2 0.7 collective-permute-start.6
  1.8 3.1 %constant_dynamic-slice_fusion = (bf16[2,1,4,64,8,128]{5,4,3,2,1,0:T(8,128)(2,1)}, bf16[2,1,4,64,8,128]{5,4,3,2,1,0:T(8,128)(2,1)}) fusion(bf16[4,2,4,128,8,128]{5,4,3,2,1,0:T(8,128)(2,1)} %bitcast.31, s32[]{:T(128)S(6)} %select_n.41, s32[]{:T(128)S(6)} %select_n.42), kind=kLoop, calls=%fused_computation.13 | loop fusion | bytes 4194312 | tf_op jit(solution)/shard_map/dynamic_slice | solution.py:292
  4.9 1.3 %collective-permute-start.3 = (bf16[8,64,8,128]{3,2,1,0:T(8,128)(2,1)}, bf16[8,64,8,128]{3,2,1,0:T(8,128)(2,1)S(1)}, u32[]{:S(2)}, u32[]{:S(2)}) collective-permute-start(bf16[8,64,8,128]{3,2,1,0:T(8,128)(2,1)} %bitcast.10), channel_id=1, source_target_pairs={{2,0},{4,2},{6,4},{10,8},{12,10},{14,12},{18,16},{20,18},{22,20},{... | collective-permute-start | bytes 3145736 | tf_op jit(solution)/shard_map/ppermute | solution.py:282
  6.2 0.7 slice_reduce_fusion.1
  6.9 6.7 %collective-permute-done.5 = s32[256,2]{0,1:T(2,128)S(1)} collective-permute-done((s32[256,2]{0,1:T(2,128)}, s32[256,2]{0,1:T(2,128)S(1)}, u32[]{:S(2)}, u32[]{:S(2)}) %collective-permute-start.5) | collective-permute-done | bytes 2080 | tf_op jit(solution)/shard_map/ppermute | solution.py:282
  13.6 0.7 collective-permute-start.1
  14.4 0.7 collective-permute-start.4
  15.1 1.6 %collective-permute-start.2 = (bf16[8,64,8,128]{3,2,1,0:T(8,128)(2,1)}, bf16[8,64,8,128]{3,2,1,0:T(8,128)(2,1)}, u32[]{:S(2)}, u32[]{:S(2)}) collective-permute-start(bf16[8,64,8,128]{3,2,1,0:T(8,128)(2,1)} %bitcast.36), channel_id=1, source_target_pairs={{1,3},{3,5},{5,7},{9,11},{11,13},{13,15},{17,19},{19,21},{21,23},{... | collective-permute-start | bytes 3145736 | tf_op jit(solution)/shard_map/ppermute | solution.py:282
  16.7 0.6 pad_add_fusion.2.where
  17.5 0.6 pad_add_fusion.where
  18.2 0.1 concatenate.23
  18.4 0.1 concatenate.19
  18.5 0.7 broadcast_select_fusion
  19.2 0.1 concatenate.22
  19.3 0.1 concatenate.21
  19.5 0.8 broadcast_in_dim.6.mask
  20.3 15.4 %local_segments.1.base = f32[16,8,72,128]{3,2,1,0:T(8,128)} custom-call(s32[2]{0:T(128)} %pad_add_fusion.2.where, bf16[32,128,8,128]{3,2,1,0:T(8,128)(2,1)} %bitcast.32, bf16[32,128,8,128]{3,2,1,0:T(8,128)(2,1)} %bitcast.7.other, f32[16,2,8,128]{3,2,1,0:T(8,128)} %broadcast_in_dim.6.mask, bf16[256,256]{1,0:T(8,128)(2,1)} %constant.50.clone.first, ...), custom_call_target="tpu_custom_call" | custom-call | tf_op jit(solution)/shard_map/local_segments/pallas_call | solution.py:336
  35.8 1.1 %broadcast_in_dim.8.weight = f32[16,6,8,128]{3,2,1,0:T(8,128)} broadcast(f32[16,6,8]{2,1,0:T(8,128)S(1)} %bitcast.37), dimensions={0,1,2} | broadcast | bytes 396288 | tf_op jit(solution)/shard_map/broadcast_in_dim | solution.py:313
  36.9 0.3 copy-done.1
  37.1 0.4 copy-done.2
  37.5 12.7 %shard_map.82 = (bf16[4,272,128]{2,1,0:T(8,128)(2,1)}, bf16[4,272,128]{2,1,0:T(8,128)(2,1)}) custom-call(s32[4]{0:T(128)} %pad_add_fusion.where, bf16[32,128,8,128]{3,2,1,0:T(8,128)(2,1)} %bitcast.33, bf16[32,128,8,128]{3,2,1,0:T(8,128)(2,1)} %bitcast.7.other, bf16[8,64,8,128]{3,2,1,0:T(8,128)(2,1)} %copy-done.1, ...), custom_call_target="tpu_custom_call" | custom-call | tf_op jit(solution)/shard_map/pallas_call | solution.py:358
  50.2 0.6 pad_add_fusion.4.where
  50.8 12.9 %shard_map.83 = (bf16[4,272,128]{2,1,0:T(8,128)(2,1)}, bf16[4,272,128]{2,1,0:T(8,128)(2,1)}) custom-call(s32[4]{0:T(128)} %pad_add_fusion.4.where, bf16[32,128,8,128]{3,2,1,0:T(8,128)(2,1)} %bitcast.34, bf16[32,128,8,128]{3,2,1,0:T(8,128)(2,1)} %bitcast.7.other, bf16[8,64,8,128]{3,2,1,0:T(8,128)(2,1)} %copy-done.1, ...), custom_call_target="tpu_custom_call" | custom-call | tf_op jit(solution)/shard_map/pallas_call | solution.py:358
  63.8 17.4 %collective-permute-start.10 = (bf16[4,272,128]{2,1,0:T(8,128)(2,1)}, bf16[4,272,128]{2,1,0:T(8,128)(2,1)S(1)}, u32[]{:S(2)}, u32[]{:S(2)}) collective-permute-start(bf16[4,272,128]{2,1,0:T(8,128)(2,1)} %get-tuple-element.13), channel_id=1, source_target_pairs={{0,6},{1,7},{2,0},{3,1},{4,2},{5,3},{6,4},{7,5},{8,14},{9,15},{10,... | collective-permute-start | bytes 835592 | tf_op jit(solution)/shard_map/ppermute | solution.py:282
  81.2 0.6 collective-permute-start.9
  81.9 6.8 %collective-permute-done.10.refs_2_ = bf16[4,272,128]{2,1,0:T(8,128)(2,1)S(1)} collective-permute-done((bf16[4,272,128]{2,1,0:T(8,128)(2,1)}, bf16[4,272,128]{2,1,0:T(8,128)(2,1)S(1)}, u32[]{:S(2)}, u32[]{:S(2)}) %collective-permute-start.10) | collective-permute-done | bytes 278560 | tf_op jit(solution)/shard_map/ppermute | solution.py:282
  88.7 14.1 %collective-permute-done.8.refs_0_ = bf16[4,272,128]{2,1,0:T(8,128)(2,1)S(1)} collective-permute-done((bf16[4,272,128]{2,1,0:T(8,128)(2,1)S(1)}, bf16[4,272,128]{2,1,0:T(8,128)(2,1)S(1)}, u32[]{:S(2)}, u32[]{:S(2)}) %collective-permute-start.8) | collective-permute-done | bytes 278560 | tf_op jit(solution)/shard_map/ppermute | solution.py:282
  102.8 0.7 copy-done.4
  103.5 0.1 copy-done.5
  103.6 2.2 %finish.1 = f32[32,4224]{1,0:T(8,128)} custom-call(bf16[4,272,128]{2,1,0:T(8,128)(2,1)} %copy-done.4, bf16[4,272,128]{2,1,0:T(8,128)(2,1)} %copy-done.5, bf16[4,272,128]{2,1,0:T(8,128)(2,1)} %copy-done.3, bf16[4,272,128]{2,1,0:T(8,128)(2,1)} %get-tuple-element.14.refs_3_, f32[33,128]{1,0:T(8,128)} %constant.55.clone.refs_4_), custom_call_target="tpu_custom_call" | custom-call | tf_op jit(solution)/shard_map/finish/pallas_call | solution.py:400
  (31 shorter events, 0.5 us)
Async XLA Ops:
  0.0 19.5 %collective-permute-start = (bf16[256,16384]{1,0:T(8,128)(2,1)}, bf16[256,16384]{1,0:T(8,128)(2,1)}, u32[]{:S(2)}, u32[]{:S(2)}) collective-permute-start(bf16[256,16384]{1,0:T(8,128)(2,1)} %param.8), channel_id=1, source_target_pairs={{0,1},{1,0},{2,3},{3,2},{4,5},{5,4},{6,7},{7,6},{8,9},{9,8},{10,11... | collective-permute-start | bytes 25165832 | tf_op jit(solution)/shard_map/ppermute | solution.py:282
  0.5 13.1 %collective-permute-start.5 = (s32[256,2]{0,1:T(2,128)}, s32[256,2]{0,1:T(2,128)S(1)}, u32[]{:S(2)}, u32[]{:S(2)}) collective-permute-start(s32[256,2]{0,1:T(2,128)} %param.9), channel_id=1, source_target_pairs={{0,1},{1,0},{2,3},{3,2},{4,5},{5,4},{6,7},{7,6},{8,9},{9,8},{10,11... | collective-permute-start | bytes 6152 | tf_op jit(solution)/shard_map/ppermute | solution.py:282
  0.5 13.8 %collective-permute-start.7 = (s32[256,2]{0,1:T(2,128)}, s32[256,2]{0,1:T(2,128)S(1)}, u32[]{:S(2)}, u32[]{:S(2)}) collective-permute-start(s32[256,2]{0,1:T(2,128)} %param.9), channel_id=1, source_target_pairs={{1,3},{3,5},{5,7},{9,11},{11,13},{13,15},{17,19},{19,21},{21,23},{... | collective-permute-start | bytes 6152 | tf_op jit(solution)/shard_map/ppermute | solution.py:282
  1.2 13.9 %collective-permute-start.6 = (s32[256,2]{0,1:T(2,128)}, s32[256,2]{0,1:T(2,128)S(1)}, u32[]{:S(2)}, u32[]{:S(2)}) collective-permute-start(s32[256,2]{0,1:T(2,128)} %param.9), channel_id=1, source_target_pairs={{1,2},{3,4},{5,6},{9,10},{11,12},{13,14},{17,18},{19,20},{21,22},{... | collective-permute-start | bytes 6152 | tf_op jit(solution)/shard_map/ppermute | solution.py:282
  4.9 30.8 %collective-permute-start.3 = (bf16[8,64,8,128]{3,2,1,0:T(8,128)(2,1)}, bf16[8,64,8,128]{3,2,1,0:T(8,128)(2,1)S(1)}, u32[]{:S(2)}, u32[]{:S(2)}) collective-permute-start(bf16[8,64,8,128]{3,2,1,0:T(8,128)(2,1)} %bitcast.10), channel_id=1, source_target_pairs={{2,0},{4,2},{6,4},{10,8},{12,10},{14,12},{18,16},{20,18},{22,20},{... | collective-permute-start | bytes 3145736 | tf_op jit(solution)/shard_map/ppermute | solution.py:282
  13.6 22.1 %collective-permute-start.1 = (bf16[8,64,8,128]{3,2,1,0:T(8,128)(2,1)}, bf16[8,64,8,128]{3,2,1,0:T(8,128)(2,1)S(1)}, u32[]{:S(2)}, u32[]{:S(2)}) collective-permute-start(bf16[8,64,8,128]{3,2,1,0:T(8,128)(2,1)} %bitcast.10), channel_id=1, source_target_pairs={{1,2},{3,4},{5,6},{9,10},{11,12},{13,14},{17,18},{19,20},{21,22},{... | collective-permute-start | bytes 3145736 | tf_op jit(solution)/shard_map/ppermute | solution.py:282
  14.4 21.4 %collective-permute-start.4 = (bf16[8,64,8,128]{3,2,1,0:T(8,128)(2,1)}, bf16[8,64,8,128]{3,2,1,0:T(8,128)(2,1)S(1)}, u32[]{:S(2)}, u32[]{:S(2)}) collective-permute-start(bf16[8,64,8,128]{3,2,1,0:T(8,128)(2,1)} %bitcast.35), channel_id=1, source_target_pairs={{2,1},{4,3},{6,5},{10,9},{12,11},{14,13},{18,17},{20,19},{22,21},{... | collective-permute-start | bytes 3145736 | tf_op jit(solution)/shard_map/ppermute | solution.py:282
  15.1 20.7 %collective-permute-start.2 = (bf16[8,64,8,128]{3,2,1,0:T(8,128)(2,1)}, bf16[8,64,8,128]{3,2,1,0:T(8,128)(2,1)}, u32[]{:S(2)}, u32[]{:S(2)}) collective-permute-start(bf16[8,64,8,128]{3,2,1,0:T(8,128)(2,1)} %bitcast.36), channel_id=1, source_target_pairs={{1,3},{3,5},{5,7},{9,11},{11,13},{13,15},{17,19},{19,21},{21,23},{... | collective-permute-start | bytes 3145736 | tf_op jit(solution)/shard_map/ppermute | solution.py:282
  35.7 1.2 %copy-start = (bf16[8,64,8,128]{3,2,1,0:T(8,128)(2,1)}, bf16[8,64,8,128]{3,2,1,0:T(8,128)(2,1)S(1)}, u32[]{:S(2)}) copy-start(bf16[8,64,8,128]{3,2,1,0:T(8,128)(2,1)S(1)} %collective-permute-done.3.upper0) | copy-start | bytes 3145732
  35.7 1.4 %copy-start.1 = (bf16[8,64,8,128]{3,2,1,0:T(8,128)(2,1)}, bf16[8,64,8,128]{3,2,1,0:T(8,128)(2,1)S(1)}, u32[]{:S(2)}) copy-start(bf16[8,64,8,128]{3,2,1,0:T(8,128)(2,1)S(1)} %collective-permute-done.1.lower0) | copy-start | bytes 3145732
  35.8 1.7 %copy-start.2 = (bf16[8,64,8,128]{3,2,1,0:T(8,128)(2,1)}, bf16[8,64,8,128]{3,2,1,0:T(8,128)(2,1)S(1)}, u32[]{:S(2)}) copy-start(bf16[8,64,8,128]{3,2,1,0:T(8,128)(2,1)S(1)} %collective-permute-done.4.upper1) | copy-start | bytes 3145732
  50.8 30.4 %copy-start.7 = (bf16[4,272,128]{2,1,0:T(8,128)(2,1)S(1)}, bf16[4,272,128]{2,1,0:T(8,128)(2,1)}, u32[]{:S(2)}) copy-start(bf16[4,272,128]{2,1,0:T(8,128)(2,1)} %get-tuple-element.10) | copy-start | bytes 835588
  50.8 30.4 %copy-start.6 = (bf16[4,272,128]{2,1,0:T(8,128)(2,1)S(1)}, bf16[4,272,128]{2,1,0:T(8,128)(2,1)}, u32[]{:S(2)}) copy-start(bf16[4,272,128]{2,1,0:T(8,128)(2,1)} %get-tuple-element.11) | copy-start | bytes 835588
  63.8 24.9 %collective-permute-start.10 = (bf16[4,272,128]{2,1,0:T(8,128)(2,1)}, bf16[4,272,128]{2,1,0:T(8,128)(2,1)S(1)}, u32[]{:S(2)}, u32[]{:S(2)}) collective-permute-start(bf16[4,272,128]{2,1,0:T(8,128)(2,1)} %get-tuple-element.13), channel_id=1, source_target_pairs={{0,6},{1,7},{2,0},{3,1},{4,2},{5,3},{6,4},{7,5},{8,14},{9,15},{10,... | collective-permute-start | bytes 835592 | tf_op jit(solution)/shard_map/ppermute | solution.py:282
  81.2 21.6 %collective-permute-start.8 = (bf16[4,272,128]{2,1,0:T(8,128)(2,1)S(1)}, bf16[4,272,128]{2,1,0:T(8,128)(2,1)S(1)}, u32[]{:S(2)}, u32[]{:S(2)}) collective-permute-start(bf16[4,272,128]{2,1,0:T(8,128)(2,1)S(1)} %copy-done.7), channel_id=1, source_target_pairs={{0,4},{1,5},{2,6},{3,7},{4,0},{5,1},{6,2},{7,3},{8,12},{9,13},{10,... | collective-permute-start | bytes 835592 | tf_op jit(solution)/shard_map/ppermute | solution.py:282
  81.2 21.6 %collective-permute-start.9 = (bf16[4,272,128]{2,1,0:T(8,128)(2,1)S(1)}, bf16[4,272,128]{2,1,0:T(8,128)(2,1)S(1)}, u32[]{:S(2)}, u32[]{:S(2)}) collective-permute-start(bf16[4,272,128]{2,1,0:T(8,128)(2,1)S(1)} %copy-done.6), channel_id=1, source_target_pairs={{0,2},{1,3},{2,4},{3,5},{4,6},{5,7},{6,0},{7,1},{8,10},{9,11},{10,... | collective-permute-start | bytes 835592 | tf_op jit(solution)/shard_map/ppermute | solution.py:282
  88.7 14.1 %copy-start.3 = (bf16[4,272,128]{2,1,0:T(8,128)(2,1)}, bf16[4,272,128]{2,1,0:T(8,128)(2,1)S(1)}, u32[]{:S(2)}) copy-start(bf16[4,272,128]{2,1,0:T(8,128)(2,1)S(1)} %collective-permute-done.10.refs_2_) | copy-start | bytes 835588
  102.8 0.7 copy-start.4
  102.8 0.8 copy-start.5
